TPU v7x, 256 devices: a whole 4x4x8 slice. The times are simulated.
256 devices in a mesh: row: 16 (over y_hi, x, core), col: 16 (over z, y_lo).
Axes of the slice: x: 4, y: 4 (y_hi: 2, y_lo: 2; y = y_hi * 2 + y_lo), z: 8, core: 2. Of those that a mesh axis runs over, the one named last changes fastest.
Arguments:
- blocks: bfloat16 [16, 16, 368, 128, 128], P('row', 'col'), may hold values from -0.125 to 0.125
- block_rows: int32 [16, 16, 368], P('row', 'col'), may hold values from 0 to 127, as said below
- block_cols: int32 [16, 16, 368], P('row', 'col'), may hold values from 0 to 127
- counts: int32 [16, 16], P('row', 'col'), may hold values from 1 to 368, as said below
- features: bfloat16 [262144, 256], P(('col', 'row')), may hold values from -6 to 6
Outputs:
- aggregated: bfloat16 [262144, 256], P(('row', 'col'))
Inputs may be any that keep to these rules, and one draw needn't show every extreme that they name: `block_rows`: within one tile the live slots name distinct pairs of block row and block column. `counts`: some tile holds exactly 368 live blocks in every draw.
All inputs are finite; a program needn't handle non-finite values.
Results may differ from a plain program's by a relative error of at most 0.013.
Values may be sent and summed in bfloat16 or wider, within the bound.
No kernel may reach another device: no remote copies, remote signals or barrier semaphores. Data moves between devices by JAX's collectives and lax.ppermute only.
A program may use at most 128 MiB of HBM per device.

v0:
```python
import jax
import jax.numpy as jnp
from jax import lax
from jax.sharding import Mesh
from jax.sharding import PartitionSpec as P

COL = ("col_0", "col_1")
COL_ROW = ("col_0", "col_1", "row")
ROW_COL = ("row", "col_0", "col_1")


def sum_by_axis(array, axes, dim):
    if not axes:
        return array
    nearer = lax.psum_scatter(array, axes[0], scatter_dimension=dim, tiled=True)
    return sum_by_axis(nearer, axes[1:], dim)


def on_device(blocks, block_rows, block_cols, counts, features):
    feature_width = features.shape[1]
    block_size = blocks.shape[-1]
    max_blocks = blocks.shape[2]
    group_size = max_blocks // 8
    row_blocks = lax.axis_size(COL) * (features.shape[0] // block_size)
    panel_rows = lax.all_gather(features, "row", axis=0, tiled=True)
    panel_blocks = panel_rows.reshape(-1, block_size, feature_width)
    tile_blocks = blocks[0, 0]
    tile_rows = block_rows[0, 0]
    tile_cols = block_cols[0, 0]
    live_count = counts[0, 0]

    def accumulate(group_index, running):
        first_slot = group_index * group_size
        weights = lax.dynamic_slice_in_dim(tile_blocks, first_slot, group_size, 0)
        rows_slice = lax.dynamic_slice_in_dim(tile_rows, first_slot, group_size, 0)
        cols_slice = lax.dynamic_slice_in_dim(tile_cols, first_slot, group_size, 0)
        positions = first_slot + jnp.arange(group_size, dtype=jnp.int32)
        weights = jnp.where(
            (positions < live_count)[:, None, None], weights, jnp.zeros_like(weights)
        )
        gathered = panel_blocks[cols_slice, :, 0:feature_width]
        product = jnp.einsum("gik,gkf->gif", weights, gathered, preferred_element_type=jnp.float32)
        return running.at[rows_slice].add(product)

    initial = jnp.zeros((row_blocks, block_size, feature_width - 0), jnp.float32)
    groups = 8
    running = lax.fori_loop(0, groups, accumulate, initial)
    summed = sum_by_axis(
        running.reshape(row_blocks * block_size, feature_width - 0).astype(jnp.bfloat16), COL, 0
    ).astype(jnp.float32)
    return summed.astype(jnp.bfloat16)


def solution(mesh):
    finer = Mesh(mesh.devices.reshape(mesh.shape["row"], 8, 2), ("row", "col_0", "col_1"))
    placed = (
        P("row", COL, None, None, None),
        P("row", COL, None),
        P("row", COL, None),
        P("row", COL),
        P(COL_ROW, None),
    )
    return jax.shard_map(
        on_device, mesh=finer, in_specs=placed, out_specs=P(ROW_COL, None), check_vma=False
    )
```

profile of v0, /device:TPU:1, one launch (start us, length us, event | category | flops | bytes accessed | tf_op | source)
XLA Modules:
  0.0 431.7 jit_solution(5214397716992773565)
XLA Ops:
  6.5 0.7 all-gather.2.cloned.1.call-update
  7.3 0.7 reduce
  8.0 0.7 reduce.1
  8.7 83.5 %all-gather.2.cloned.1.call-done = bf16[16384,256]{1,0:T(8,128)(2,1)} async-done(((bf16[1024,256]{1,0:T(8,128)(2,1)}), bf16[16384,256]{1,0:T(8,128)(2,1)}) %all-gather.2.cloned.1.call-update) | async-done | bytes 8388624 | tf_op jit(solution)/shard_map/all_gather | solution.py:25
  92.2 7.8 %broadcast_in_dim.38 = f32[128,128,256]{2,1,0:T(8,128)} broadcast(f32[]{:T(128)} %constant.44.clone.1), dimensions={} | broadcast | bytes 16777220 | tf_op jit(solution)/shard_map/broadcast_in_dim | solution.py:45
  100.0 196.8 %while.13 = (s32[]{:T(128)}, f32[128,128,256]{2,1,0:T(8,128)}, s32[368]{0:T(512)S(1)}, s32[]{:T(128)}, bf16[368,128,128]{2,1,0:T(8,128)(2,1)}, /*index=5*/s32[36...) while((s32[]{:T(128)}, f32[128,128,256]{2,1,0:T(8,128)}, ...), condition=%wide.region_2.3_spmd, body=%wide.region_0.2_spmd.sunk | while | flops 388138368 | bytes 34674192 | solution.py:47
  100.0 0.7 add_compare_fusion.2
  100.6 0.1 compare_select_fusion.3
  100.7 4.1 gather_fusion
  104.9 5.0 %fusion.13 = f32[46,128,256]{2,1,0:T(8,128)} fusion(bf16[46,128,256]{2,1,0:T(8,128)(2,1)S(1)} %gather_fusion, bf16[368,128,128]{2,1,0:T(8,128)(2,1)} %get-tuple-element.219, s32[]{:T(128)S(6)} %select_n.40, pred[46]{0:T(512)(128)(4,1)S(1)} %add_compare_fusion.2), kind=kOutput, calls=%fused_computation.2.clone.1 | convolution fusion | flops 386629632 | bytes 10551346 | tf_op jit(solution)/shard_map/while/body/eval_jaxpr/gik,gkf->gif/dot_general | solution.py:42
  109.9 14.8 %scatter_fusion = f32[128,128,256]{2,1,0:T(8,128)} fusion(f32[128,128,256]{2,1,0:T(8,128)} %get-tuple-element.205, s32[46]{0:T(128)S(1)} %get-tuple-element.191, f32[46,128,256]{2,1,0:T(8,128)} %fusion.13), kind=kCustom, calls=%fused_computation.1.clone.1 | custom fusion | flops 1507328 | bytes 18088120 | tf_op jit(solution)/shard_map/while/body/eval_jaxpr/scatter-add | solution.py:43
  124.6 0.7 add_compare_fusion.2
  125.3 0.1 compare_select_fusion.3
  125.4 4.1 gather_fusion
  129.5 5.0 %fusion.13 = f32[46,128,256]{2,1,0:T(8,128)} fusion(bf16[46,128,256]{2,1,0:T(8,128)(2,1)S(1)} %gather_fusion, bf16[368,128,128]{2,1,0:T(8,128)(2,1)} %get-tuple-element.219, s32[]{:T(128)S(6)} %select_n.40, pred[46]{0:T(512)(128)(4,1)S(1)} %add_compare_fusion.2), kind=kOutput, calls=%fused_computation.2.clone.1 | convolution fusion | flops 386629632 | bytes 10551346 | tf_op jit(solution)/shard_map/while/body/eval_jaxpr/gik,gkf->gif/dot_general | solution.py:42
  134.5 14.7 %scatter_fusion = f32[128,128,256]{2,1,0:T(8,128)} fusion(f32[128,128,256]{2,1,0:T(8,128)} %get-tuple-element.205, s32[46]{0:T(128)S(1)} %get-tuple-element.191, f32[46,128,256]{2,1,0:T(8,128)} %fusion.13), kind=kCustom, calls=%fused_computation.1.clone.1 | custom fusion | flops 1507328 | bytes 18088120 | tf_op jit(solution)/shard_map/while/body/eval_jaxpr/scatter-add | solution.py:43
  149.3 0.7 add_compare_fusion.2
  149.9 0.1 compare_select_fusion.3
  150.0 4.1 gather_fusion
  154.1 5.0 %fusion.13 = f32[46,128,256]{2,1,0:T(8,128)} fusion(bf16[46,128,256]{2,1,0:T(8,128)(2,1)S(1)} %gather_fusion, bf16[368,128,128]{2,1,0:T(8,128)(2,1)} %get-tuple-element.219, s32[]{:T(128)S(6)} %select_n.40, pred[46]{0:T(512)(128)(4,1)S(1)} %add_compare_fusion.2), kind=kOutput, calls=%fused_computation.2.clone.1 | convolution fusion | flops 386629632 | bytes 10551346 | tf_op jit(solution)/shard_map/while/body/eval_jaxpr/gik,gkf->gif/dot_general | solution.py:42
  159.2 14.7 %scatter_fusion = f32[128,128,256]{2,1,0:T(8,128)} fusion(f32[128,128,256]{2,1,0:T(8,128)} %get-tuple-element.205, s32[46]{0:T(128)S(1)} %get-tuple-element.191, f32[46,128,256]{2,1,0:T(8,128)} %fusion.13), kind=kCustom, calls=%fused_computation.1.clone.1 | custom fusion | flops 1507328 | bytes 18088120 | tf_op jit(solution)/shard_map/while/body/eval_jaxpr/scatter-add | solution.py:43
  173.8 0.7 add_compare_fusion.2
  174.5 0.1 compare_select_fusion.3
  174.6 4.1 gather_fusion
  178.7 5.0 %fusion.13 = f32[46,128,256]{2,1,0:T(8,128)} fusion(bf16[46,128,256]{2,1,0:T(8,128)(2,1)S(1)} %gather_fusion, bf16[368,128,128]{2,1,0:T(8,128)(2,1)} %get-tuple-element.219, s32[]{:T(128)S(6)} %select_n.40, pred[46]{0:T(512)(128)(4,1)S(1)} %add_compare_fusion.2), kind=kOutput, calls=%fused_computation.2.clone.1 | convolution fusion | flops 386629632 | bytes 10551346 | tf_op jit(solution)/shard_map/while/body/eval_jaxpr/gik,gkf->gif/dot_general | solution.py:42
  183.7 14.7 %scatter_fusion = f32[128,128,256]{2,1,0:T(8,128)} fusion(f32[128,128,256]{2,1,0:T(8,128)} %get-tuple-element.205, s32[46]{0:T(128)S(1)} %get-tuple-element.191, f32[46,128,256]{2,1,0:T(8,128)} %fusion.13), kind=kCustom, calls=%fused_computation.1.clone.1 | custom fusion | flops 1507328 | bytes 18088120 | tf_op jit(solution)/shard_map/while/body/eval_jaxpr/scatter-add | solution.py:43
  198.4 0.7 add_compare_fusion.2
  199.1 0.1 compare_select_fusion.3
  199.2 4.1 gather_fusion
  203.3 5.0 %fusion.13 = f32[46,128,256]{2,1,0:T(8,128)} fusion(bf16[46,128,256]{2,1,0:T(8,128)(2,1)S(1)} %gather_fusion, bf16[368,128,128]{2,1,0:T(8,128)(2,1)} %get-tuple-element.219, s32[]{:T(128)S(6)} %select_n.40, pred[46]{0:T(512)(128)(4,1)S(1)} %add_compare_fusion.2), kind=kOutput, calls=%fused_computation.2.clone.1 | convolution fusion | flops 386629632 | bytes 10551346 | tf_op jit(solution)/shard_map/while/body/eval_jaxpr/gik,gkf->gif/dot_general | solution.py:42
  208.3 14.7 %scatter_fusion = f32[128,128,256]{2,1,0:T(8,128)} fusion(f32[128,128,256]{2,1,0:T(8,128)} %get-tuple-element.205, s32[46]{0:T(128)S(1)} %get-tuple-element.191, f32[46,128,256]{2,1,0:T(8,128)} %fusion.13), kind=kCustom, calls=%fused_computation.1.clone.1 | custom fusion | flops 1507328 | bytes 18088120 | tf_op jit(solution)/shard_map/while/body/eval_jaxpr/scatter-add | solution.py:43
  223.0 0.7 add_compare_fusion.2
  223.6 0.1 compare_select_fusion.3
  223.7 4.1 gather_fusion
  227.8 5.0 %fusion.13 = f32[46,128,256]{2,1,0:T(8,128)} fusion(bf16[46,128,256]{2,1,0:T(8,128)(2,1)S(1)} %gather_fusion, bf16[368,128,128]{2,1,0:T(8,128)(2,1)} %get-tuple-element.219, s32[]{:T(128)S(6)} %select_n.40, pred[46]{0:T(512)(128)(4,1)S(1)} %add_compare_fusion.2), kind=kOutput, calls=%fused_computation.2.clone.1 | convolution fusion | flops 386629632 | bytes 10551346 | tf_op jit(solution)/shard_map/while/body/eval_jaxpr/gik,gkf->gif/dot_general | solution.py:42
  232.8 14.7 %scatter_fusion = f32[128,128,256]{2,1,0:T(8,128)} fusion(f32[128,128,256]{2,1,0:T(8,128)} %get-tuple-element.205, s32[46]{0:T(128)S(1)} %get-tuple-element.191, f32[46,128,256]{2,1,0:T(8,128)} %fusion.13), kind=kCustom, calls=%fused_computation.1.clone.1 | custom fusion | flops 1507328 | bytes 18088120 | tf_op jit(solution)/shard_map/while/body/eval_jaxpr/scatter-add | solution.py:43
  247.5 0.7 add_compare_fusion.2
  248.2 0.1 compare_select_fusion.3
  248.3 4.1 gather_fusion
  252.4 5.0 %fusion.13 = f32[46,128,256]{2,1,0:T(8,128)} fusion(bf16[46,128,256]{2,1,0:T(8,128)(2,1)S(1)} %gather_fusion, bf16[368,128,128]{2,1,0:T(8,128)(2,1)} %get-tuple-element.219, s32[]{:T(128)S(6)} %select_n.40, pred[46]{0:T(512)(128)(4,1)S(1)} %add_compare_fusion.2), kind=kOutput, calls=%fused_computation.2.clone.1 | convolution fusion | flops 386629632 | bytes 10551346 | tf_op jit(solution)/shard_map/while/body/eval_jaxpr/gik,gkf->gif/dot_general | solution.py:42
  257.4 14.7 %scatter_fusion = f32[128,128,256]{2,1,0:T(8,128)} fusion(f32[128,128,256]{2,1,0:T(8,128)} %get-tuple-element.205, s32[46]{0:T(128)S(1)} %get-tuple-element.191, f32[46,128,256]{2,1,0:T(8,128)} %fusion.13), kind=kCustom, calls=%fused_computation.1.clone.1 | custom fusion | flops 1507328 | bytes 18088120 | tf_op jit(solution)/shard_map/while/body/eval_jaxpr/scatter-add | solution.py:43
  272.1 0.7 add_compare_fusion.2
  272.9 4.1 gather_fusion
  277.0 5.0 %fusion.13 = f32[46,128,256]{2,1,0:T(8,128)} fusion(bf16[46,128,256]{2,1,0:T(8,128)(2,1)S(1)} %gather_fusion, bf16[368,128,128]{2,1,0:T(8,128)(2,1)} %get-tuple-element.219, s32[]{:T(128)S(6)} %select_n.40, pred[46]{0:T(512)(128)(4,1)S(1)} %add_compare_fusion.2), kind=kOutput, calls=%fused_computation.2.clone.1 | convolution fusion | flops 386629632 | bytes 10551346 | tf_op jit(solution)/shard_map/while/body/eval_jaxpr/gik,gkf->gif/dot_general | solution.py:42
  282.0 14.8 %scatter_fusion = f32[128,128,256]{2,1,0:T(8,128)} fusion(f32[128,128,256]{2,1,0:T(8,128)} %get-tuple-element.205, s32[46]{0:T(128)S(1)} %get-tuple-element.191, f32[46,128,256]{2,1,0:T(8,128)} %fusion.13), kind=kCustom, calls=%fused_computation.1.clone.1 | custom fusion | flops 1507328 | bytes 18088120 | tf_op jit(solution)/shard_map/while/body/eval_jaxpr/scatter-add | solution.py:43
  296.8 9.0 %convert_element_type.8 = bf16[128,128,256]{2,1,0:T(8,128)(2,1)} convert(f32[128,128,256]{2,1,0:T(8,128)} %get-tuple-element.129) | non-fusion elementwise | flops 4194304 | bytes 25165824 | tf_op jit(solution)/shard_map/convert_element_type | solution.py:49
  305.9 92.8 %reduce-scatter.3.cloned.1.call-done = bf16[2048,256]{1,0:T(8,128)(2,1)} async-done(((bf16[16384,256]{1,0:T(8,128)(2,1)}), bf16[2048,256]{1,0:T(8,128)(2,1)}) %reduce-scatter.3.cloned.1.call-update) | async-done | bytes 1048592 | tf_op jit(solution)/shard_map/reduce_scatter | solution.py:15
  398.7 26.5 %reduce-scatter.5.cloned.1.call-done = bf16[1024,256]{1,0:T(8,128)(2,1)} async-done(((bf16[2048,256]{1,0:T(8,128)(2,1)}), bf16[1024,256]{1,0:T(8,128)(2,1)}) %reduce-scatter.5.cloned.1.call-update) | async-done | bytes 524304 | tf_op jit(solution)/shard_map/reduce_scatter | solution.py:15
  (14 shorter events, 0.2 us)
Async XLA Ops:
  6.5 85.6 %all-gather.2.cloned.1.call-start = ((), (), s32[]{:S(2)}) async-start(), calls=%async_computation.2 | async-start | bytes 8912896 | tf_op jit(solution)/shard_map/all_gather | solution.py:25
  7.3 391.4 %reduce-scatter.3.cloned.1.call-start = ((), (), s32[]{:S(2)}) async-start(), calls=%async_computation.3 | async-start | bytes 9437184 | tf_op jit(solution)/shard_map/reduce_scatter | solution.py:15
  305.8 119.3 %reduce-scatter.5.cloned.1.call-start = ((), (), s32[]{:S(2)}) async-start(), calls=%async_computation.4 | async-start | bytes 1572864 | tf_op jit(solution)/shard_map/reduce_scatter | solution.py:15
Sparse Core Ops, SparseCore 0:
  10.1 82.0 all-gather.1
  305.9 92.6 reduce-scatter.2
  401.1 23.9 reduce-scatter.4
where the time goes:
time: 433 us; the launch traced here: 432 us
  waiting for transfers between devices  203 us (47%)
  other arithmetic  134 us (31%)
  local copies, waits for them, and re-layouts  40.8 us (9%)
  matrix products  40.1 us (9%)
  between operations  13.1 us (3%)
    reduce_scatter x2, waiting for transfers between devices, sum_by_axis(): nearer = lax.psum_scatter(array, axes[0], scatter_dimension=dim, tiled=True)  119 us
    scatter-add x8, other arithmetic, accumulate(): return running.at[rows_slice].add(product)  118 us
    all_gather x1, waiting for transfers between devices, on_device(): panel_rows = lax.all_gather(features, 'row', axis=0, tiled=True)  83.5 us
    dot_general x8, matrix products, accumulate(): jnp.einsum('gik,gkf->gif', weights, gathered, preferred_element_type=jnp....  40.1 us
    gather x8, local copies, waits for them, and re-layouts, accumulate(): gathered = panel_blocks[cols_slice, :, 0:feature_width]  33 us
    convert_element_type x1, other arithmetic, on_device(): running.reshape(row_blocks * block_size, feature_width - 0)  9.02 us
  transfers between devices with their start and end apart: 3, of which 3 were waited for; matrix products, arithmetic and copies ran while one was open for 0% of the time, Pallas kernels for 0%

commit v1 on v0

--- a/solution.py
+++ b/solution.py
@@ -22,7 +22,9 @@
     max_blocks = blocks.shape[2]
     group_size = max_blocks // 8
     row_blocks = lax.axis_size(COL) * (features.shape[0] // block_size)
-    panel_rows = lax.all_gather(features, "row", axis=0, tiled=True)
+    panel_rows = jnp.concatenate(
+        lax.all_to_all(jnp.stack([features] * lax.axis_size("row")), "row", 0, 0), axis=0
+    )
     panel_blocks = panel_rows.reshape(-1, block_size, feature_width)
     tile_blocks = blocks[0, 0]
     tile_rows = block_rows[0, 0]

time: 433 us -> 478 us (1.10)
  waiting for transfers between devices: 203 us -> 236 us
  starting transfers between devices: 0.08 us -> 8.64 us
  local copies, waits for them, and re-layouts: 40.8 us -> 45.9 us
    all_to_all x0 -> x1, waiting for transfers between devices: none -> 112 us  [on_device(): lax.all_to_all(jnp.stack([features] * lax.axis_size('row')), 'row', 0, 0)]
    all_gather x1 -> x0, waiting for transfers between devices: 83.5 us -> none  [on_device(): panel_rows = lax.all_gather(features, 'row', axis=0, tiled=True)]
    all_to_all x0 -> x1, starting transfers between devices: none -> 8.57 us  [on_device(): lax.all_to_all(jnp.stack([features] * lax.axis_size('row')), 'row', 0, 0)]
    another operation x0 -> x1, local copies, waits for them, and re-layouts: none -> 5.07 us  [on_device(): jnp.stack([features] * lax.axis_size('row'))]
where the time goes in v1:
time: 478 us; the launch traced here: 477 us
  waiting for transfers between devices  236 us (49%)
  other arithmetic  133 us (28%)
  local copies, waits for them, and re-layouts  45.9 us (10%)
  matrix products  40.1 us (8%)
  between operations  13.4 us (3%)
  starting transfers between devices  8.64 us (2%)
    reduce_scatter x2, waiting for transfers between devices, sum_by_axis(): nearer = lax.psum_scatter(array, axes[0], scatter_dimension=dim, tiled=True)  123 us
    scatter-add x8, other arithmetic, accumulate(): return running.at[rows_slice].add(product)  118 us
    all_to_all x1, waiting for transfers between devices, on_device(): lax.all_to_all(jnp.stack([features] * lax.axis_size('row')), 'row', 0, 0)  112 us
    dot_general x8, matrix products, accumulate(): jnp.einsum('gik,gkf->gif', weights, gathered, preferred_element_type=jnp....  40.1 us
    gather x8, local copies, waits for them, and re-layouts, accumulate(): gathered = panel_blocks[cols_slice, :, 0:feature_width]  33 us
  transfers between devices with their start and end apart: 3, of which 3 were waited for; matrix products, arithmetic and copies ran while one was open for 0% of the time, Pallas kernels for 0%

profile of v1, /device:TPU:1, one launch (start us, length us, event | category | flops | bytes accessed | tf_op | source)
XLA Modules:
  0.0 476.6 jit_solution(15375631132397673037)
XLA Ops:
  6.5 5.1 %stack.2 = bf16[16,1024,256]{2,1,0:T(8,128)(2,1)} broadcast(bf16[1024,256]{1,0:T(8,128)(2,1)} %param.11), dimensions={1,2} | broadcast | bytes 8912896 | tf_op jit(solution)/shard_map/stack | solution.py:26
  11.6 8.6 %all-to-all-start = ((bf16[16,1024,256]{2,1,0:T(8,128)(2,1)}), bf16[16,1024,256]{2,1,0:T(8,128)(2,1)}, u32[]{:S(2)}, u32[]{:S(2)}) async-start(bf16[16,1024,256]{2,1,0:T(8,128)(2,1)} %stack.2), calls=%async_computation | async-start | bytes 16777216 | tf_op jit(solution)/shard_map/all_to_all | solution.py:26
  20.3 112.4 %all-to-all-done = bf16[16,1024,256]{2,1,0:T(8,128)(2,1)} async-done(((bf16[16,1024,256]{2,1,0:T(8,128)(2,1)}), bf16[16,1024,256]{2,1,0:T(8,128)(2,1)}, u32[]{:S(2)}, u32[]{:S(2)}) %all-to-all-start) | async-done | bytes 8388640 | tf_op jit(solution)/shard_map/all_to_all | solution.py:26
  132.6 7.8 %broadcast_in_dim.38 = f32[128,128,256]{2,1,0:T(8,128)} broadcast(f32[]{:T(128)} %constant.44.clone.1), dimensions={} | broadcast | bytes 16777220 | tf_op jit(solution)/shard_map/broadcast_in_dim | solution.py:47
  140.5 196.8 %while.13 = (s32[]{:T(128)}, f32[128,128,256]{2,1,0:T(8,128)}, s32[368]{0:T(512)S(1)}, s32[]{:T(128)}, bf16[368,128,128]{2,1,0:T(8,128)(2,1)}, /*index=5*/s32[36...) while((s32[]{:T(128)}, f32[128,128,256]{2,1,0:T(8,128)}, ...), condition=%wide.region_2.3_spmd, body=%wide.region_0.2_spmd.sunk | while | flops 388138368 | bytes 34674192 | solution.py:49
  140.5 0.7 add_compare_fusion.2
  141.1 0.1 compare_select_fusion.3
  141.2 4.1 gather_fusion
  145.3 5.0 %fusion.13 = f32[46,128,256]{2,1,0:T(8,128)} fusion(bf16[46,128,256]{2,1,0:T(8,128)(2,1)S(1)} %gather_fusion, bf16[368,128,128]{2,1,0:T(8,128)(2,1)} %get-tuple-element.219, s32[]{:T(128)S(6)} %select_n.40, pred[46]{0:T(512)(128)(4,1)S(1)} %add_compare_fusion.2), kind=kOutput, calls=%fused_computation.2.clone.1 | convolution fusion | flops 386629632 | bytes 10551346 | tf_op jit(solution)/shard_map/while/body/eval_jaxpr/gik,gkf->gif/dot_general | solution.py:44
  150.3 14.8 %scatter_fusion = f32[128,128,256]{2,1,0:T(8,128)} fusion(f32[128,128,256]{2,1,0:T(8,128)} %get-tuple-element.205, s32[46]{0:T(128)S(1)} %get-tuple-element.191, f32[46,128,256]{2,1,0:T(8,128)} %fusion.13), kind=kCustom, calls=%fused_computation.1.clone.1 | custom fusion | flops 1507328 | bytes 18088120 | tf_op jit(solution)/shard_map/while/body/eval_jaxpr/scatter-add | solution.py:45
  165.1 0.7 add_compare_fusion.2
  165.8 0.1 compare_select_fusion.3
  165.9 4.1 gather_fusion
  170.0 5.0 %fusion.13 = f32[46,128,256]{2,1,0:T(8,128)} fusion(bf16[46,128,256]{2,1,0:T(8,128)(2,1)S(1)} %gather_fusion, bf16[368,128,128]{2,1,0:T(8,128)(2,1)} %get-tuple-element.219, s32[]{:T(128)S(6)} %select_n.40, pred[46]{0:T(512)(128)(4,1)S(1)} %add_compare_fusion.2), kind=kOutput, calls=%fused_computation.2.clone.1 | convolution fusion | flops 386629632 | bytes 10551346 | tf_op jit(solution)/shard_map/while/body/eval_jaxpr/gik,gkf->gif/dot_general | solution.py:44
  175.0 14.7 %scatter_fusion = f32[128,128,256]{2,1,0:T(8,128)} fusion(f32[128,128,256]{2,1,0:T(8,128)} %get-tuple-element.205, s32[46]{0:T(128)S(1)} %get-tuple-element.191, f32[46,128,256]{2,1,0:T(8,128)} %fusion.13), kind=kCustom, calls=%fused_computation.1.clone.1 | custom fusion | flops 1507328 | bytes 18088120 | tf_op jit(solution)/shard_map/while/body/eval_jaxpr/scatter-add | solution.py:45
  189.7 0.7 add_compare_fusion.2
  190.4 0.1 compare_select_fusion.3
  190.5 4.1 gather_fusion
  194.6 5.0 %fusion.13 = f32[46,128,256]{2,1,0:T(8,128)} fusion(bf16[46,128,256]{2,1,0:T(8,128)(2,1)S(1)} %gather_fusion, bf16[368,128,128]{2,1,0:T(8,128)(2,1)} %get-tuple-element.219, s32[]{:T(128)S(6)} %select_n.40, pred[46]{0:T(512)(128)(4,1)S(1)} %add_compare_fusion.2), kind=kOutput, calls=%fused_computation.2.clone.1 | convolution fusion | flops 386629632 | bytes 10551346 | tf_op jit(solution)/shard_map/while/body/eval_jaxpr/gik,gkf->gif/dot_general | solution.py:44
  199.6 14.7 %scatter_fusion = f32[128,128,256]{2,1,0:T(8,128)} fusion(f32[128,128,256]{2,1,0:T(8,128)} %get-tuple-element.205, s32[46]{0:T(128)S(1)} %get-tuple-element.191, f32[46,128,256]{2,1,0:T(8,128)} %fusion.13), kind=kCustom, calls=%fused_computation.1.clone.1 | custom fusion | flops 1507328 | bytes 18088120 | tf_op jit(solution)/shard_map/while/body/eval_jaxpr/scatter-add | solution.py:45
  214.3 0.7 add_compare_fusion.2
  214.9 0.1 compare_select_fusion.3
  215.0 4.1 gather_fusion
  219.2 5.0 %fusion.13 = f32[46,128,256]{2,1,0:T(8,128)} fusion(bf16[46,128,256]{2,1,0:T(8,128)(2,1)S(1)} %gather_fusion, bf16[368,128,128]{2,1,0:T(8,128)(2,1)} %get-tuple-element.219, s32[]{:T(128)S(6)} %select_n.40, pred[46]{0:T(512)(128)(4,1)S(1)} %add_compare_fusion.2), kind=kOutput, calls=%fused_computation.2.clone.1 | convolution fusion | flops 386629632 | bytes 10551346 | tf_op jit(solution)/shard_map/while/body/eval_jaxpr/gik,gkf->gif/dot_general | solution.py:44
  224.2 14.7 %scatter_fusion = f32[128,128,256]{2,1,0:T(8,128)} fusion(f32[128,128,256]{2,1,0:T(8,128)} %get-tuple-element.205, s32[46]{0:T(128)S(1)} %get-tuple-element.191, f32[46,128,256]{2,1,0:T(8,128)} %fusion.13), kind=kCustom, calls=%fused_computation.1.clone.1 | custom fusion | flops 1507328 | bytes 18088120 | tf_op jit(solution)/shard_map/while/body/eval_jaxpr/scatter-add | solution.py:45
  238.9 0.7 add_compare_fusion.2
  239.5 0.1 compare_select_fusion.3
  239.6 4.1 gather_fusion
  243.8 5.0 %fusion.13 = f32[46,128,256]{2,1,0:T(8,128)} fusion(bf16[46,128,256]{2,1,0:T(8,128)(2,1)S(1)} %gather_fusion, bf16[368,128,128]{2,1,0:T(8,128)(2,1)} %get-tuple-element.219, s32[]{:T(128)S(6)} %select_n.40, pred[46]{0:T(512)(128)(4,1)S(1)} %add_compare_fusion.2), kind=kOutput, calls=%fused_computation.2.clone.1 | convolution fusion | flops 386629632 | bytes 10551346 | tf_op jit(solution)/shard_map/while/body/eval_jaxpr/gik,gkf->gif/dot_general | solution.py:44
  248.8 14.7 %scatter_fusion = f32[128,128,256]{2,1,0:T(8,128)} fusion(f32[128,128,256]{2,1,0:T(8,128)} %get-tuple-element.205, s32[46]{0:T(128)S(1)} %get-tuple-element.191, f32[46,128,256]{2,1,0:T(8,128)} %fusion.13), kind=kCustom, calls=%fused_computation.1.clone.1 | custom fusion | flops 1507328 | bytes 18088120 | tf_op jit(solution)/shard_map/while/body/eval_jaxpr/scatter-add | solution.py:45
  263.4 0.7 add_compare_fusion.2
  264.1 0.1 compare_select_fusion.3
  264.2 4.1 gather_fusion
  268.3 5.0 %fusion.13 = f32[46,128,256]{2,1,0:T(8,128)} fusion(bf16[46,128,256]{2,1,0:T(8,128)(2,1)S(1)} %gather_fusion, bf16[368,128,128]{2,1,0:T(8,128)(2,1)} %get-tuple-element.219, s32[]{:T(128)S(6)} %select_n.40, pred[46]{0:T(512)(128)(4,1)S(1)} %add_compare_fusion.2), kind=kOutput, calls=%fused_computation.2.clone.1 | convolution fusion | flops 386629632 | bytes 10551346 | tf_op jit(solution)/shard_map/while/body/eval_jaxpr/gik,gkf->gif/dot_general | solution.py:44
  273.3 14.7 %scatter_fusion = f32[128,128,256]{2,1,0:T(8,128)} fusion(f32[128,128,256]{2,1,0:T(8,128)} %get-tuple-element.205, s32[46]{0:T(128)S(1)} %get-tuple-element.191, f32[46,128,256]{2,1,0:T(8,128)} %fusion.13), kind=kCustom, calls=%fused_computation.1.clone.1 | custom fusion | flops 1507328 | bytes 18088120 | tf_op jit(solution)/shard_map/while/body/eval_jaxpr/scatter-add | solution.py:45
  288.0 0.7 add_compare_fusion.2
  288.7 0.1 compare_select_fusion.3
  288.8 4.1 gather_fusion
  292.9 5.0 %fusion.13 = f32[46,128,256]{2,1,0:T(8,128)} fusion(bf16[46,128,256]{2,1,0:T(8,128)(2,1)S(1)} %gather_fusion, bf16[368,128,128]{2,1,0:T(8,128)(2,1)} %get-tuple-element.219, s32[]{:T(128)S(6)} %select_n.40, pred[46]{0:T(512)(128)(4,1)S(1)} %add_compare_fusion.2), kind=kOutput, calls=%fused_computation.2.clone.1 | convolution fusion | flops 386629632 | bytes 10551346 | tf_op jit(solution)/shard_map/while/body/eval_jaxpr/gik,gkf->gif/dot_general | solution.py:44
  297.9 14.7 %scatter_fusion = f32[128,128,256]{2,1,0:T(8,128)} fusion(f32[128,128,256]{2,1,0:T(8,128)} %get-tuple-element.205, s32[46]{0:T(128)S(1)} %get-tuple-element.191, f32[46,128,256]{2,1,0:T(8,128)} %fusion.13), kind=kCustom, calls=%fused_computation.1.clone.1 | custom fusion | flops 1507328 | bytes 18088120 | tf_op jit(solution)/shard_map/while/body/eval_jaxpr/scatter-add | solution.py:45
  312.6 0.7 add_compare_fusion.2
  313.2 0.1 compare_select_fusion.3
  313.3 4.1 gather_fusion
  317.5 5.0 %fusion.13 = f32[46,128,256]{2,1,0:T(8,128)} fusion(bf16[46,128,256]{2,1,0:T(8,128)(2,1)S(1)} %gather_fusion, bf16[368,128,128]{2,1,0:T(8,128)(2,1)} %get-tuple-element.219, s32[]{:T(128)S(6)} %select_n.40, pred[46]{0:T(512)(128)(4,1)S(1)} %add_compare_fusion.2), kind=kOutput, calls=%fused_computation.2.clone.1 | convolution fusion | flops 386629632 | bytes 10551346 | tf_op jit(solution)/shard_map/while/body/eval_jaxpr/gik,gkf->gif/dot_general | solution.py:44
  322.5 14.8 %scatter_fusion = f32[128,128,256]{2,1,0:T(8,128)} fusion(f32[128,128,256]{2,1,0:T(8,128)} %get-tuple-element.205, s32[46]{0:T(128)S(1)} %get-tuple-element.191, f32[46,128,256]{2,1,0:T(8,128)} %fusion.13), kind=kCustom, calls=%fused_computation.1.clone.1 | custom fusion | flops 1507328 | bytes 18088120 | tf_op jit(solution)/shard_map/while/body/eval_jaxpr/scatter-add | solution.py:45
  337.3 9.0 %convert_element_type.8 = bf16[128,128,256]{2,1,0:T(8,128)(2,1)} convert(f32[128,128,256]{2,1,0:T(8,128)} %get-tuple-element.129) | non-fusion elementwise | flops 4194304 | bytes 25165824 | tf_op jit(solution)/shard_map/convert_element_type | solution.py:51
  346.3 96.9 %reduce-scatter.3.cloned.1.call-done = bf16[2048,256]{1,0:T(8,128)(2,1)} async-done(((bf16[16384,256]{1,0:T(8,128)(2,1)}), bf16[2048,256]{1,0:T(8,128)(2,1)}) %reduce-scatter.3.cloned.1.call-update) | async-done | bytes 1048592 | tf_op jit(solution)/shard_map/reduce_scatter | solution.py:15
  443.2 26.5 %reduce-scatter.5.cloned.1.call-done = bf16[1024,256]{1,0:T(8,128)(2,1)} async-done(((bf16[2048,256]{1,0:T(8,128)(2,1)}), bf16[1024,256]{1,0:T(8,128)(2,1)}) %reduce-scatter.5.cloned.1.call-update) | async-done | bytes 524304 | tf_op jit(solution)/shard_map/reduce_scatter | solution.py:15
  (18 shorter events, 0.2 us)
Async XLA Ops:
  11.6 8.6 %copy-start = (s32[1,1,368]{2,1,0:T(1,128)S(1)}, s32[1,1,368]{2,1,0:T(1,128)}, u32[]{:S(2)}) copy-start(s32[1,1,368]{2,1,0:T(1,128)} %param.8) | copy-start | bytes 4420
  11.6 8.6 %copy-start.1 = (s32[1,1,368]{2,1,0:T(1,128)S(1)}, s32[1,1,368]{2,1,0:T(1,128)}, u32[]{:S(2)}) copy-start(s32[1,1,368]{2,1,0:T(1,128)} %param.9) | copy-start | bytes 4420
  11.6 121.0 %all-to-all-start = ((bf16[16,1024,256]{2,1,0:T(8,128)(2,1)}), bf16[16,1024,256]{2,1,0:T(8,128)(2,1)}, u32[]{:S(2)}, u32[]{:S(2)}) async-start(bf16[16,1024,256]{2,1,0:T(8,128)(2,1)} %stack.2), calls=%async_computation | async-start | bytes 16777216 | tf_op jit(solution)/shard_map/all_to_all | solution.py:26
  20.2 423.0 %reduce-scatter.3.cloned.1.call-start = ((), (), s32[]{:S(2)}) async-start(), calls=%async_computation.3 | async-start | bytes 9437184 | tf_op jit(solution)/shard_map/reduce_scatter | solution.py:15
  346.3 123.4 %reduce-scatter.5.cloned.1.call-start = ((), (), s32[]{:S(2)}) async-start(), calls=%async_computation.4 | async-start | bytes 1572864 | tf_op jit(solution)/shard_map/reduce_scatter | solution.py:15
Sparse Core Ops, SparseCore 0:
  346.4 96.7 reduce-scatter.2
  445.7 23.9 reduce-scatter.4
